TPU v7x, 32 devices: a whole 2x2x4 slice. The times are simulated.
32 devices in a mesh: row: 16 (over z, x, core), col: 2 (over y).
Axes of the slice: x: 2, y: 2, z: 4, core: 2. Of those that a mesh axis runs over, the one named last changes fastest.
Arguments:
- joined: bfloat16 [2, 64, 16, 28, 4096], P(None, None, 'row', None, 'col'), may hold values from -0.09375 to 0.09375
- probes: bfloat16 [2, 128, 4096], P(None, None, 'col'), may hold values from -6 to 6
Outputs:
- gate_rows: bfloat16 [2, 14336, 4096], P(None, 'row', 'col')
- up_rows: bfloat16 [2, 14336, 4096], P(None, 'row', 'col')
- hidden: bfloat16 [2, 128, 14336], P(None, 'col', 'row')
All inputs are finite; a program needn't handle non-finite values.
Results may differ from a plain program's by a relative error of at most 0.002.
Values may be sent and summed in bfloat16 or wider, within the bound.
A program may use at most 128 MiB of HBM per device.

v0:
```python
import jax
import jax.numpy as jnp
from jax import lax
from jax.sharding import PartitionSpec as P


def own_rows(portion, extent, axis):
    count = extent * lax.axis_size(axis)
    return lax.psum_scatter(portion(jnp.int32(0), count), axis, scatter_dimension=0, tiled=True)


def make_term(probe_layer, gate_layer, up_layer):

    def partial_term(first_row, row_count):
        probe_rows = lax.dynamic_slice_in_dim(probe_layer, first_row, row_count, 0)
        gate_part = jnp.dot(probe_rows, gate_layer.T, preferred_element_type=jnp.float32)
        up_part = jnp.dot(probe_rows, up_layer.T, preferred_element_type=jnp.float32)
        return jnp.concatenate((gate_part, up_part), axis=1)

    return partial_term


def per_device(joined, probes):
    layers = joined.shape[0]
    cycles = joined.shape[1]
    block_rows = joined.shape[3]
    columns = joined.shape[4]
    peer_count = lax.axis_size("row")
    groups = cycles // peer_count
    half_rows = block_rows // 2
    outgoing = joined.reshape(layers, peer_count, groups, block_rows, columns)
    arrived = lax.all_to_all(outgoing, "row", split_axis=1, concat_axis=1, tiled=True)
    separated = arrived.reshape(layers, peer_count, groups, half_rows, 2, columns)
    rows_own = peer_count * groups * half_rows
    gate_rows = (
        separated[:, :, :, :, 0, :].transpose(0, 2, 1, 3, 4).reshape(layers, rows_own, columns)
    )
    up_rows = (
        separated[:, :, :, :, 1, :].transpose(0, 2, 1, 3, 4).reshape(layers, rows_own, columns)
    )
    row_share = probes.shape[1] // lax.axis_size("col")
    results = []
    for layer_index in range(layers):
        partial_term = make_term(probes[layer_index], gate_rows[layer_index], up_rows[layer_index])
        summed = own_rows(partial_term, row_share, "col")
        results.append(
            (jax.nn.silu(summed[:, :rows_own]) * summed[:, rows_own:]).astype(jnp.bfloat16)
        )
    hidden = jnp.stack(results, axis=0)
    return (gate_rows, up_rows, hidden)


def solution(mesh):
    in_specs = (P(None, None, "row", None, "col"), P(None, None, "col"))
    out_specs = (P(None, "row", "col"), P(None, "row", "col"), P(None, "col", "row"))
    return jax.shard_map(
        per_device, mesh=mesh, in_specs=in_specs, out_specs=out_specs, check_vma=False
    )
```

profile of v0, /device:TPU:0, one launch (start us, length us, event | category | flops | bytes accessed | tf_op | source)
XLA Modules:
  0.0 491.4 jit_solution(15821664690213613716)
XLA Ops:
  7.2 26.7 %copy.13 = bf16[2,64,1,28,2048]{4,0,3,1,2:T(2,128)(2,1)S(1)} copy(bf16[2,64,1,28,2048]{4,1,3,2,0:T(8,128)(2,1)} %param.2) | data formatting | bytes 29360128 | tf_op args[0]
  33.9 324.8 %all_to_all.5 = bf16[2,16,4,28,2048]{4,0,3,2,1:T(2,128)(2,1)S(1)} all-to-all(bf16[2,16,4,28,2048]{4,0,3,2,1:T(2,128)(2,1)S(1)} %bitcast.33), channel_id=1, replica_groups=mesh['row'=16,'col'=2] {'row'}, dimensions={1} | all-to-all | bytes 29360128 | tf_op jit(solution)/shard_map/all_to_all | solution.py:32
  358.7 10.1 %copy.14 = bf16[2,16,4,28,2048]{4,1,3,2,0:T(8,128)(2,1)} copy(bf16[2,16,4,28,2048]{4,0,3,2,1:T(2,128)(2,1)S(1)} %all_to_all.5) | data formatting | bytes 29360128 | tf_op jit(solution)/shard_map/all_to_all | solution.py:32
  368.8 6.4 %slice_bitcast_fusion = (bf16[2,4,16,14,2048]{4,2,3,1,0:T(8,128)(2,1)S(1)}, bf16[2,4,16,14,2048]{4,2,3,1,0:T(8,128)(2,1)S(1)}) fusion(bf16[2,16,4,14,2,2048]{5,1,4,3,2,0:T(8,128)(2,1)} %bitcast.32), kind=kLoop, calls=%fused_computation | loop fusion | bytes 29360128 | tf_op jit(solution)/shard_map/transpose | solution.py:39
  375.2 4.9 fusion.16
  380.1 1.5 copy-done
  381.5 2.4 copy-done.1
  384.0 4.0 copy.18
  387.9 5.9 %squeeze.28 = bf16[896,2048]{1,0:T(8,128)(2,1)} reshape(bf16[1,4,16,14,2048]{4,3,2,1,0:T(8,128)(2,1)} %copy.18) | data formatting | bytes 7340032 | tf_op jit(solution)/shard_map/squeeze | solution.py:44
  393.9 6.1 %copy.17 = bf16[1,4,16,14,2048]{4,3,2,1,0:T(8,128)(2,1)} copy(bf16[1,4,16,14,2048]{4,2,3,1,0:T(8,128)(2,1)} %get-tuple-element.11) | data formatting | bytes 7340032 | tf_op jit(solution)/shard_map/slice | solution.py:44
  400.0 6.1 %squeeze.27 = bf16[896,2048]{1,0:T(8,128)(2,1)} reshape(bf16[1,4,16,14,2048]{4,3,2,1,0:T(8,128)(2,1)} %copy.17) | data formatting | bytes 7340032 | tf_op jit(solution)/shard_map/squeeze | solution.py:44
  406.1 3.5 fusion.4
  409.6 1.3 fusion.6
  412.1 6.1 %copy.20 = bf16[1,4,16,14,2048]{4,3,2,1,0:T(8,128)(2,1)} copy(bf16[1,4,16,14,2048]{4,2,3,1,0:T(8,128)(2,1)} %get-tuple-element.15) | data formatting | bytes 7340032 | tf_op jit(solution)/shard_map/slice | solution.py:44
  418.2 5.9 %squeeze.31 = bf16[896,2048]{1,0:T(8,128)(2,1)} reshape(bf16[1,4,16,14,2048]{4,3,2,1,0:T(8,128)(2,1)} %copy.20) | data formatting | bytes 7340032 | tf_op jit(solution)/shard_map/squeeze | solution.py:44
  424.1 6.1 %copy.19 = bf16[1,4,16,14,2048]{4,3,2,1,0:T(8,128)(2,1)} copy(bf16[1,4,16,14,2048]{4,2,3,1,0:T(8,128)(2,1)} %get-tuple-element.12) | data formatting | bytes 7340032 | tf_op jit(solution)/shard_map/slice | solution.py:44
  430.2 6.0 %squeeze.30 = bf16[896,2048]{1,0:T(8,128)(2,1)} reshape(bf16[1,4,16,14,2048]{4,3,2,1,0:T(8,128)(2,1)} %copy.19) | data formatting | bytes 7340032 | tf_op jit(solution)/shard_map/squeeze | solution.py:44
  436.2 3.5 fusion
  439.7 1.3 fusion.2
  442.0 15.0 %copy.15 = bf16[2,4,16,14,2048]{4,0,3,2,1:T(2,128)(2,1)} copy(bf16[2,4,16,14,2048]{4,2,3,1,0:T(8,128)(2,1)} %copy-done.1) | data formatting | bytes 14680064 | tf_op jit(solution)/shard_map/transpose | solution.py:36
  457.0 8.3 %copy.16 = bf16[2,4,16,14,2048]{4,0,3,2,1:T(2,128)(2,1)} copy(bf16[2,4,16,14,2048]{4,2,3,1,0:T(8,128)(2,1)S(1)} %bitcast.31) | data formatting | bytes 14680064 | tf_op jit(solution)/shard_map/transpose | solution.py:39
  465.3 9.8 %copy.21 = bf16[2,896,2048]{2,1,0:T(8,128)(2,1)} copy(bf16[2,896,2048]{2,0,1:T(2,128)(2,1)} %bitcast.34) | data formatting | bytes 14680064
  475.1 6.4 %copy.22 = bf16[2,896,2048]{2,1,0:T(8,128)(2,1)} copy(bf16[2,896,2048]{2,0,1:T(2,128)(2,1)S(1)} %bitcast.35) | data formatting | bytes 14680064
  482.7 1.1 fusion.15
  (25 shorter events, 4.2 us)
Async XLA Ops:
  7.2 474.4 %reduce-scatter.3.cloned.1.call-start = ((), (), s32[]{:S(2)}) async-start(), calls=%async_computation.3 | async-start | bytes 1376256 | tf_op jit(solution)/shard_map/reduce_scatter | solution.py:9
  375.2 6.4 %copy-start = (bf16[2,4,16,14,2048]{4,2,3,1,0:T(8,128)(2,1)}, bf16[2,4,16,14,2048]{4,2,3,1,0:T(8,128)(2,1)S(1)}, u32[]{:S(2)}) copy-start(bf16[2,4,16,14,2048]{4,2,3,1,0:T(8,128)(2,1)S(1)} %get-tuple-element.9) | copy-start | bytes 22020100
  375.2 8.8 %copy-start.1 = (bf16[2,4,16,14,2048]{4,2,3,1,0:T(8,128)(2,1)}, bf16[2,4,16,14,2048]{4,2,3,1,0:T(8,128)(2,1)S(1)}, u32[]{:S(2)}) copy-start(bf16[2,4,16,14,2048]{4,2,3,1,0:T(8,128)(2,1)S(1)} %get-tuple-element.10) | copy-start | bytes 22020100
  400.0 6.1 %copy-start.5 = (bf16[2,128,2048]{2,1,0:T(8,128)(2,1)S(1)}, bf16[2,128,2048]{2,1,0:T(8,128)(2,1)}, u32[]{:S(2)}) copy-start(bf16[2,128,2048]{2,1,0:T(8,128)(2,1)} %param.3) | copy-start | bytes 3145732
  406.1 3.5 copy-start.3
  411.9 70.8 %reduce-scatter.5.cloned.1.call-start = ((), (), s32[]{:S(2)}) async-start(), calls=%async_computation.4 | async-start | bytes 1376256 | tf_op jit(solution)/shard_map/reduce_scatter | solution.py:9
  436.2 3.5 copy-start.4
  440.9 16.0 %slice-start = ((s8[7340032]{0:T(1024)(128)(4,1)}), s8[3145728]{0:T(1024)(128)(4,1)S(1)}, s32[]{:S(2)}) async-start(s8[7340032]{0:T(1024)(128)(4,1)} %bitcast.30), calls=%async_computation.5 | async-start | bytes 6291456
  442.0 15.0 %slice-start.1 = ((s8[7340032]{0:T(1024)(128)(4,1)}), s8[4194304]{0:T(1024)(128)(4,1)S(1)}, s32[]{:S(2)}) async-start(s8[7340032]{0:T(1024)(128)(4,1)} %bitcast.30), calls=%async_computation.6 | async-start | bytes 8388608
  465.3 9.8 %copy-start.2 = (bf16[2,4,16,14,2048]{4,0,3,2,1:T(2,128)(2,1)S(1)}, bf16[2,4,16,14,2048]{4,0,3,2,1:T(2,128)(2,1)}, u32[]{:S(2)}) copy-start(bf16[2,4,16,14,2048]{4,0,3,2,1:T(2,128)(2,1)} %copy.16) | copy-start | bytes 22020100
Sparse Core Ops, SparseCore 0:
  412.0 18.4 reduce-scatter.2
  442.1 18.4 reduce-scatter.4
where the time goes:
time: 492 us; the launch traced here: 491 us
  blocking collectives  325 us (66%)
  local copies, waits for them, and re-layouts  138 us (28%)
  between operations  14.2 us (3%)
  matrix products  9.48 us (2%)
  other arithmetic  4.97 us (1%)
    all_to_all x1, blocking collectives, per_device(): lax.all_to_all(outgoing, 'row', split_axis=1, concat_axis=1, tiled=True)  325 us
    unnamed x19, local copies, waits for them, and re-layouts  46.8 us
    slice x3, local copies, waits for them, and re-layouts, per_device(): gate_rows[layer_index]  17.1 us
    transpose x1, local copies, waits for them, and re-layouts, per_device(): separated[:, :, :, :, 0, :].transpose(0, 2, 1, 3, 4)  15 us
    transpose x2, local copies, waits for them, and re-layouts, per_device(): separated[:, :, :, :, 1, :].transpose(0, 2, 1, 3, 4)  14.7 us
    squeeze x2, local copies, waits for them, and re-layouts, per_device(): gate_rows[layer_index]  12.1 us
    squeeze x2, local copies, waits for them, and re-layouts, per_device(): up_rows[layer_index]  11.8 us
    slice x2, local copies, waits for them, and re-layouts, per_device(): up_rows[layer_index]  10.1 us
  transfers between devices with their start and end apart: 2, of which 0 were waited for; matrix products, arithmetic and copies ran while one was open for 14% of the time, Pallas kernels for 0%

commit v1 on v0

v1 whole, which is shorter than its diff:
```python
import functools

import jax
import jax.numpy as jnp
import numpy as np
from jax import lax
from jax.experimental import pallas as pl
from jax.experimental.pallas import tpu as pltpu
from jax.sharding import PartitionSpec as P

MESH = pl.DeviceIdType.MESH
BAND = 16
PEERS = 8


def pack_matrix(groups, block_rows, slot):
    half = block_rows // 2
    dests = BAND // groups
    out = np.zeros((dests * slot, block_rows * BAND), np.float32)
    for q in range(dests):
        for h in range(2):
            for g in range(groups):
                for r in range(half):
                    out[q * slot + (h * groups + g) * half + r, (2 * r + h) * BAND + q * groups + g] = 1
    return out


def unpack_matrix(groups, block_rows, slot):
    half = block_rows // 2
    out = np.zeros((2 * groups * PEERS * half, PEERS * slot), np.float32)
    for h in range(2):
        for g in range(groups):
            for p in range(PEERS):
                for r in range(half):
                    out[((h * groups + g) * PEERS + p) * half + r, p * slot + (h * groups + g) * half + r] = 1
    return out


def kernel(
    n, m, groups, slot, pieces,
    joined, probes, pack, unpack, gate_out, up_out, hidden,
    loaded, packed, landed, stage, acc, others,
    load_sem, send_sem, recv_sem, own_sem, out_sem, ysend_sem, yrecv_sem,
):
    layers, block_rows, cycles, _ = joined.shape
    width = loaded.shape[-1]
    half = block_rows // 2
    rows_own = n * groups * half
    me = lax.axis_index("row")
    mine = lax.axis_index("col")
    chunks = layers * pieces

    def load(c):
        return pltpu.make_async_copy(
            joined.at[c // pieces, :, :, pl.ds((c % pieces) * width, width)], loaded.at[c], load_sem.at[c]
        )

    for c in range(chunks):
        load(c).start()

    barrier = pltpu.get_barrier_semaphore()

    def greet(i, carry):
        pl.semaphore_signal(barrier, inc=1, device_id={"row": lax.rem(me + i, n)}, device_id_type=MESH)
        return carry

    lax.fori_loop(1, n, greet, 0)
    for i in range(1, m):
        pl.semaphore_signal(barrier, inc=1, device_id={"col": lax.rem(mine + i, m)}, device_id_type=MESH)
    pl.semaphore_wait(barrier, n - 1 + m - 1)

    def rows_of(q):
        return pl.ds(pl.multiple_of(q * slot, 16), slot)

    def remote(c, off):
        to = lax.rem(me + off, n)
        return pltpu.make_async_remote_copy(
            src_ref=packed.at[c, rows_of(to)],
            dst_ref=landed.at[c, rows_of(me)],
            send_sem=send_sem.at[c, off],
            recv_sem=recv_sem.at[c, off],
            device_id={"row": to},
            device_id_type=MESH,
        )

    def arrival(c, off):
        src = lax.rem(me - off + n, n)
        return pltpu.make_async_remote_copy(
            src_ref=packed.at[c, rows_of(src)],
            dst_ref=landed.at[c, rows_of(src)],
            send_sem=send_sem.at[c, off],
            recv_sem=recv_sem.at[c, off],
            device_id={"row": lax.rem(me + off, n)},
            device_id_type=MESH,
        )

    def own(c):
        return pltpu.make_async_copy(packed.at[c, rows_of(me)], landed.at[c, rows_of(me)], own_sem.at[c])

    band_out = (BAND // groups) * slot
    for c in range(chunks):
        load(c).wait()

        def pack_band(j, carry):
            band = loaded[c, :, pl.ds(pl.multiple_of(j * BAND, BAND), BAND), :]
            band = band.reshape(block_rows * BAND, width)
            moved = jnp.dot(pack[...], band, preferred_element_type=jnp.float32)
            packed[c, pl.ds(pl.multiple_of(j * band_out, 16), band_out), :] = moved.astype(jnp.bfloat16)
            return carry

        lax.fori_loop(0, cycles // BAND, pack_band, 0)

        def send(i, carry):
            remote(c, 1 + lax.rem(n // 2 - 1 + i, n - 1)).start()
            return carry

        lax.fori_loop(0, n - 1, send, 0)
        own(c).start()

    def outs(c):
        columns = pl.ds((c % pieces) * width, width)
        return [
            pltpu.make_async_copy(stage.at[c % 2, h], ref.at[c // pieces, :, columns], out_sem.at[c % 2, h])
            for h, ref in ((0, gate_out), (1, up_out))
        ]

    def partial_copy(layer, i):
        to = lax.rem(mine + i, m)
        return pltpu.make_async_remote_copy(
            src_ref=acc.at[layer, to],
            dst_ref=others.at[layer, i - 1],
            send_sem=ysend_sem.at[layer, i - 1],
            recv_sem=yrecv_sem.at[layer, i - 1],
            device_id={"col": to},
            device_id_type=MESH,
        )

    def finish(layer):
        total = acc[layer, mine]
        for i in range(1, m):
            partial_copy(layer, i).wait()
            total = total + others[layer, i - 1]
        gate = total[:, :rows_own]
        hidden[layer] = (gate / (1.0 + jnp.exp(-gate)) * total[:, rows_own:]).astype(jnp.bfloat16)

    for c in range(chunks):
        layer, piece = c // pieces, c % pieces
        if c >= 2:
            for copy in outs(c - 2):
                copy.wait()
        own(c).wait()

        def land(off, carry):
            arrival(c, off).wait_recv()
            return carry

        lax.fori_loop(1, n, land, 0)

        def unpack_peers(j, carry):
            start = pl.multiple_of(j * PEERS * slot, 16)
            moved = jnp.dot(
                unpack[...], landed[c, pl.ds(start, PEERS * slot), :], preferred_element_type=jnp.float32
            ).astype(jnp.bfloat16)
            size = PEERS * half
            for h in range(2):
                for g in range(groups):
                    first = pl.multiple_of(g * n * half + j * size, 16)
                    at = (h * groups + g) * size
                    stage[c % 2, h, pl.ds(first, size), :] = moved[at : at + size]
            return carry

        lax.fori_loop(0, n // PEERS, unpack_peers, 0)
        for copy in outs(c):
            copy.start()
        probe = probes[layer, :, piece * width : (piece + 1) * width]
        for h in range(2):
            part = lax.dot_general(
                probe, stage[c % 2, h], (((1,), (1,)), ((), ())), preferred_element_type=jnp.float32
            ).reshape(m, -1, rows_own)
            span = slice(h * rows_own, (h + 1) * rows_own)
            if piece == 0:
                acc[layer, :, :, span] = part
            else:
                acc[layer, :, :, span] += part
        if piece == pieces - 1:
            for i in range(1, m):
                partial_copy(layer, i).start()
        if c == chunks - 2:
            for early in range(layers - 1 if pieces > 1 else 0):
                finish(early)
    for late in range(layers - 1 if pieces > 1 else 0, layers):
        finish(late)
    for c in range(max(chunks - 2, 0), chunks):
        for copy in outs(c):
            copy.wait()
    for c in range(chunks):

        def sent(off, carry):
            remote(c, off).wait_send()
            return carry

        lax.fori_loop(1, n, sent, 0)


def per_device(joined, probes):
    layers, cycles, _, block_rows, columns = joined.shape
    n, m = lax.axis_size("row"), lax.axis_size("col")
    groups = cycles // n
    slot = -(-groups * block_rows // 16) * 16
    width = min(columns, 512)
    pieces = columns // width
    chunks = layers * pieces
    half = block_rows // 2
    rows_own = n * groups * half
    tokens = probes.shape[1]
    by_row = joined.transpose(0, 3, 2, 1, 4).reshape(layers, block_rows, cycles, columns)
    pack = jnp.asarray(pack_matrix(groups, block_rows, slot), jnp.bfloat16)
    unpack = jnp.asarray(unpack_matrix(groups, block_rows, slot), jnp.bfloat16)
    vmem = pl.BlockSpec(memory_space=pltpu.VMEM)
    anywhere = pl.BlockSpec(memory_space=pl.ANY)
    share = tokens // m
    weight = jax.ShapeDtypeStruct((layers, rows_own, columns), jnp.bfloat16)
    return pl.pallas_call(
        functools.partial(kernel, n, m, groups, slot, pieces),
        out_shape=(weight, weight, jax.ShapeDtypeStruct((layers, share, rows_own), jnp.bfloat16)),
        in_specs=[anywhere, vmem, vmem, vmem],
        out_specs=(anywhere, anywhere, vmem),
        scratch_shapes=[
            pltpu.VMEM((chunks, block_rows, cycles, width), jnp.bfloat16),
            pltpu.VMEM((chunks, n * slot, width), jnp.bfloat16),
            pltpu.VMEM((chunks, n * slot, width), jnp.bfloat16),
            pltpu.VMEM((2, 2, rows_own, width), jnp.bfloat16),
            pltpu.VMEM((layers, m, share, 2 * rows_own), jnp.float32),
            pltpu.VMEM((layers, max(m - 1, 1), share, 2 * rows_own), jnp.float32),
            pltpu.SemaphoreType.DMA((chunks,)),
            pltpu.SemaphoreType.DMA((chunks, n)),
            pltpu.SemaphoreType.DMA((chunks, n)),
            pltpu.SemaphoreType.DMA((chunks,)),
            pltpu.SemaphoreType.DMA((2, 2)),
            pltpu.SemaphoreType.DMA((layers, max(m - 1, 1))),
            pltpu.SemaphoreType.DMA((layers, max(m - 1, 1))),
        ],
        compiler_params=pltpu.CompilerParams(
            collective_id=0, has_side_effects=True, vmem_limit_bytes=62 * 2**20
        ),
        name="redistribute",
    )(by_row, probes, pack, unpack)


def solution(mesh):
    in_specs = (P(None, None, "row", None, "col"), P(None, None, "col"))
    out_specs = (P(None, "row", "col"), P(None, "row", "col"), P(None, "col", "row"))
    return jax.shard_map(
        per_device, mesh=mesh, in_specs=in_specs, out_specs=out_specs, check_vma=False
    )
```

time: 492 us -> 357 us (0.73)
  Pallas kernels: 0 us -> 345 us
  blocking collectives: 325 us -> 0 us
  local copies, waits for them, and re-layouts: 138 us -> 11.4 us
  between operations: 14.2 us -> 0.65 us
  matrix products: 9.48 us -> 0 us
  other arithmetic: 4.97 us -> 0 us
    pallas_call x0 -> x1, Pallas kernels: none -> 345 us  [per_device(): pl.pallas_call(functools.partial(kernel, n, m, groups, slot, pieces), out...]
    all_to_all x1 -> x0, blocking collectives: 325 us -> none  [per_device(): lax.all_to_all(outgoing, 'row', split_axis=1, concat_axis=1, tiled=True)]
    unnamed x19 -> x7, local copies, waits for them, and re-layouts: 46.8 us -> 11.4 us
    transpose x3 -> x0, local copies, waits for them, and re-layouts: 29.6 us -> none  [the longest x1 15 us: per_device(): separated[:, :, :, :, 0, :].transpose(0, 2, 1, 3, 4)]
    slice x5 -> x0, local copies, waits for them, and re-layouts: 27.2 us -> none  [the longest x3 17.1 us: per_device(): gate_rows[layer_index]]
    squeeze x4 -> x0, local copies, waits for them, and re-layouts: 23.9 us -> none  [the longest x2 12.1 us: per_device(): gate_rows[layer_index]]
    all_to_all x1 -> x0, local copies, waits for them, and re-layouts: 10.1 us -> none  [per_device(): lax.all_to_all(outgoing, 'row', split_axis=1, concat_axis=1, tiled=True)]
    dot_general x4 -> x0, matrix products: 9.48 us -> none  [the longest x2 6.93 us: partial_term(): jnp.dot(probe_rows, up_layer.T, preferred_element_type=jnp.float32)]
  transfers between devices with their start and end apart: 2 -> 0, of which waited for: 0 -> 0; matrix products, arithmetic and copies ran while one was open for 14% -> 0% of each run, Pallas kernels for 0% -> 0%
where the time goes in v1:
time: 357 us
  Pallas kernels  345 us (97%)
  local copies, waits for them, and re-layouts  11.4 us (3%)
    pallas_call x1, Pallas kernels, per_device(): pl.pallas_call(functools.partial(kernel, n, m, groups, slot, pieces), out...  345 us
    unnamed x7, local copies, waits for them, and re-layouts  11.4 us

profile of v1, /device:TPU:0, one launch (start us, length us, event | category | flops | bytes accessed | tf_op | source)
XLA Modules:
  0.0 356.8 jit_solution(17997601015021093348)
XLA Ops:
  0.6 344.8 %redistribute.1 = (bf16[2,896,2048]{2,1,0:T(8,128)(2,1)}, bf16[2,896,2048]{2,1,0:T(8,128)(2,1)}, bf16[2,64,896]{2,1,0:T(8,128)(2,1)}) custom-call(bf16[2,28,64,2048]{3,2,1,0:T(8,128)(2,1)} %bitcast.5, bf16[2,128,2048]{2,1,0:T(8,128)(2,1)} %probes.1, bf16[448,448]{1,0:T(8,128)(2,1)} %constant.4.clone.pack, bf16[896,896]{1,0:T(8,128)(2,1)} %constant.5.clone.unpack), custom_call_target="tpu_custom_call" | custom-call | tf_op jit(solution)/shard_map/redistribute/pallas_call | solution.py:223
  345.4 0.0 copy-start
  345.4 7.7 %copy.11 = bf16[2,896,2048]{2,1,0:T(8,128)(2,1)} copy(bf16[2,896,2048]{2,1,0:T(8,128)(2,1)} %get-tuple-element.6) | data formatting | bytes 14680064
  353.1 0.0 copy-done
  353.1 0.0 copy-start.1
  353.1 3.0 copy.12
  356.1 0.0 copy-done.1
  356.1 0.7 copy.13
Async XLA Ops:
  345.4 7.7 %copy-start = (bf16[2,896,2048]{2,1,0:T(8,128)(2,1)S(1)}, bf16[2,896,2048]{2,1,0:T(8,128)(2,1)}, u32[]{:S(2)}) copy-start(bf16[2,896,2048]{2,1,0:T(8,128)(2,1)} %get-tuple-element.7) | copy-start | bytes 22020100
  353.1 3.1 copy-start.1

commit v2 on v1

--- a/solution.py
+++ b/solution.py
@@ -38,10 +38,11 @@
 
 def kernel(
     n, m, groups, slot, pieces,
-    joined, probes, pack, unpack, gate_out, up_out, hidden,
-    loaded, packed, landed, stage, acc, others,
-    load_sem, send_sem, recv_sem, own_sem, out_sem, ysend_sem, yrecv_sem,
+    joined, probes, pack, unpack, gate_out, up_out, hidden, *rest,
 ):
+    partial_outs = rest[:m]
+    loaded, packed, landed, stage, acc, others = rest[m : m + 6]
+    load_sem, send_sem, recv_sem, own_sem, out_sem, ysend_sem, yrecv_sem, part_sem = rest[m + 6 :]
     layers, block_rows, cycles, _ = joined.shape
     width = loaded.shape[-1]
     half = block_rows // 2
@@ -182,14 +183,22 @@
                 acc[layer, :, :, span] = part
             else:
                 acc[layer, :, :, span] += part
-        if piece == pieces - 1:
+        if piece == pieces - 1 and layer < layers - 1:
             for i in range(1, m):
                 partial_copy(layer, i).start()
         if c == chunks - 2:
             for early in range(layers - 1 if pieces > 1 else 0):
                 finish(early)
-    for late in range(layers - 1 if pieces > 1 else 0, layers):
+    hand_over = [
+        pltpu.make_async_copy(acc.at[layers - 1, lax.rem(mine + i, m)], partial_outs[i], part_sem.at[i])
+        for i in range(m)
+    ]
+    for copy in hand_over:
+        copy.start()
+    for late in range(layers - 1 if pieces > 1 else 0, layers - 1):
         finish(late)
+    for copy in hand_over:
+        copy.wait()
     for c in range(max(chunks - 2, 0), chunks):
         for copy in outs(c):
             copy.wait()
@@ -200,6 +209,29 @@
             return carry
 
         lax.fori_loop(1, n, sent, 0)
+
+
+def settle(*refs):
+    half = len(refs) // 2
+    for source, target in zip(refs[:half], refs[half:]):
+        target[...] = source[...]
+
+
+def settled(*arrays):
+    layers, rows, columns = arrays[0].shape
+    height = rows // 2
+    spec = pl.BlockSpec((1, height, columns), lambda i, j: (i, j, 0))
+    moved = 2 * sum(a.size * a.dtype.itemsize for a in arrays)
+    return pl.pallas_call(
+        settle,
+        grid=(layers, 2),
+        in_specs=[spec] * len(arrays),
+        out_specs=[spec] * len(arrays),
+        out_shape=[jax.ShapeDtypeStruct(a.shape, a.dtype) for a in arrays],
+        cost_estimate=pl.CostEstimate(flops=0, bytes_accessed=moved, transcendentals=0),
+        compiler_params=pltpu.CompilerParams(vmem_limit_bytes=62 * 2**20),
+        name="settle",
+    )(*arrays)
 
 
 def per_device(joined, probes):
@@ -220,31 +252,40 @@
     anywhere = pl.BlockSpec(memory_space=pl.ANY)
     share = tokens // m
     weight = jax.ShapeDtypeStruct((layers, rows_own, columns), jnp.bfloat16)
-    return pl.pallas_call(
+    early = layers - 1
+    partial = jax.ShapeDtypeStruct((share, 2 * rows_own), jnp.float32)
+    gate_rows, up_rows, hidden, kept, *given = pl.pallas_call(
         functools.partial(kernel, n, m, groups, slot, pieces),
-        out_shape=(weight, weight, jax.ShapeDtypeStruct((layers, share, rows_own), jnp.bfloat16)),
+        out_shape=(weight, weight, jax.ShapeDtypeStruct((early, share, rows_own), jnp.bfloat16), *[partial] * m),
         in_specs=[anywhere, vmem, vmem, vmem],
-        out_specs=(anywhere, anywhere, vmem),
+        out_specs=(anywhere, anywhere, vmem, *[anywhere] * m),
         scratch_shapes=[
             pltpu.VMEM((chunks, block_rows, cycles, width), jnp.bfloat16),
             pltpu.VMEM((chunks, n * slot, width), jnp.bfloat16),
             pltpu.VMEM((chunks, n * slot, width), jnp.bfloat16),
             pltpu.VMEM((2, 2, rows_own, width), jnp.bfloat16),
             pltpu.VMEM((layers, m, share, 2 * rows_own), jnp.float32),
-            pltpu.VMEM((layers, max(m - 1, 1), share, 2 * rows_own), jnp.float32),
+            pltpu.VMEM((early, max(m - 1, 1), share, 2 * rows_own), jnp.float32),
             pltpu.SemaphoreType.DMA((chunks,)),
             pltpu.SemaphoreType.DMA((chunks, n)),
             pltpu.SemaphoreType.DMA((chunks, n)),
             pltpu.SemaphoreType.DMA((chunks,)),
             pltpu.SemaphoreType.DMA((2, 2)),
-            pltpu.SemaphoreType.DMA((layers, max(m - 1, 1))),
-            pltpu.SemaphoreType.DMA((layers, max(m - 1, 1))),
+            pltpu.SemaphoreType.DMA((early, max(m - 1, 1))),
+            pltpu.SemaphoreType.DMA((early, max(m - 1, 1))),
+            pltpu.SemaphoreType.DMA((m,)),
         ],
         compiler_params=pltpu.CompilerParams(
             collective_id=0, has_side_effects=True, vmem_limit_bytes=62 * 2**20
         ),
         name="redistribute",
     )(by_row, probes, pack, unpack)
+    total = kept
+    for i, term in enumerate(given, 1):
+        total = total + lax.ppermute(term, "col", [(q, (q + i) % m) for q in range(m)])
+    gate = total[:, :rows_own]
+    last = (jax.nn.silu(gate) * total[:, rows_own:]).astype(jnp.bfloat16)
+    return *settled(gate_rows, up_rows), jnp.concatenate((hidden, last[None]), axis=0)
 
 
 def solution(mesh):

time: 357 us -> 348 us (0.975)
  local copies, waits for them, and re-layouts: 11.4 us -> 0.01 us
    pallas_call x1, Pallas kernels: 345 us -> 333 us  [per_device(): pl.pallas_call(functools.partial(kernel, n, m, groups, slot, pieces), out...]
    unnamed x7 -> x4, local copies, waits for them, and re-layouts: 11.4 us -> 0.01 us
    pallas_call x0 -> x1, Pallas kernels: none -> 10.5 us  [settled(): pl.pallas_call(settle, grid=(layers, 2), in_specs=[spec] * len(arrays), o...]
  transfers between devices with their start and end apart: 0 -> 1, of which waited for: 0 -> 1; matrix products, arithmetic and copies ran while one was open for 0% -> 0% of each run, Pallas kernels for 0% -> 3%
where the time goes in v2:
time: 348 us
  Pallas kernels  343 us (99%)
    pallas_call x1, Pallas kernels, per_device(): pl.pallas_call(functools.partial(kernel, n, m, groups, slot, pieces), out...  333 us
    pallas_call x1, Pallas kernels, settled(): pl.pallas_call(settle, grid=(layers, 2), in_specs=[spec] * len(arrays), o...  10.5 us
  transfers between devices with their start and end apart: 1, of which 1 were waited for; matrix products, arithmetic and copies ran while one was open for 0% of the time, Pallas kernels for 3%

profile of v2, /device:TPU:0, one launch (start us, length us, event | category | flops | bytes accessed | tf_op | source)
XLA Modules:
  0.0 347.6 jit_solution(2910835256508559715)
XLA Ops:
  0.6 332.8 %redistribute.1 = (bf16[2,896,2048]{2,1,0:T(8,128)(2,1)}, bf16[2,896,2048]{2,1,0:T(8,128)(2,1)}, bf16[1,64,896]{2,1,0:T(8,128)(2,1)}, f32[64,1792]{1,0:T(8,128)}, f32[64,1792]{1,0:T(8,128)}) custom-call(bf16[2,28,64,2048]{3,2,1,0:T(8,128)(2,1)} %bitcast.7, bf16[2,128,2048]{2,1,0:T(8,128)(2,1)} %probes.1, bf16[448,448]{1,0:T(8,128)(2,1)} %constant.7.clone.pack, ...), custom_call_target="tpu_custom_call" | custom-call | tf_op jit(solution)/shard_map/redistribute/pallas_call | solution.py:257
  333.4 1.5 collective-permute-start
  334.9 0.0 copy-start
  334.9 0.0 copy-start.1
  334.9 10.5 %settle.1 = (bf16[2,896,2048]{2,1,0:T(8,128)(2,1)}, bf16[2,896,2048]{2,1,0:T(8,128)(2,1)}) custom-call(bf16[2,896,2048]{2,1,0:T(8,128)(2,1)} %get-tuple-element.10.refs_0_, bf16[2,896,2048]{2,1,0:T(8,128)(2,1)} %get-tuple-element.11.refs_1_), custom_call_target="tpu_custom_call" | custom-call | bytes 29360128 | tf_op jit(solution)/shard_map/settle/pallas_call | solution.py:225
  345.4 1.3 collective-permute-done
  346.7 0.0 copy-done
  346.8 0.1 fusion.1
  346.9 0.0 copy-done.1
  346.9 0.7 pad_maximum_fusion
  (1 shorter events, 0.0 us)
Async XLA Ops:
  333.4 13.3 %collective-permute-start = (f32[64,1792]{1,0:T(8,128)}, f32[64,1792]{1,0:T(8,128)S(1)}, u32[]{:S(2)}, u32[]{:S(2)}) collective-permute-start(f32[64,1792]{1,0:T(8,128)} %get-tuple-element.16), channel_id=1, source_target_pairs={{0,1},{1,0},{2,3},{3,2},{4,5},{5,4},{6,7},{7,6},{8,9},{9,8},{10,11... | collective-permute-start | bytes 1376264 | tf_op jit(solution)/shard_map/ppermute | solution.py:285
  334.9 11.8 %copy-start = (f32[64,1792]{1,0:T(8,128)S(1)}, f32[64,1792]{1,0:T(8,128)}, u32[]{:S(2)}) copy-start(f32[64,1792]{1,0:T(8,128)} %get-tuple-element.15) | copy-start | bytes 1376260
  334.9 11.9 %copy-start.1 = (bf16[1,64,896]{2,1,0:T(8,128)(2,1)S(1)}, bf16[1,64,896]{2,1,0:T(8,128)(2,1)}, u32[]{:S(2)}) copy-start(bf16[1,64,896]{2,1,0:T(8,128)(2,1)} %get-tuple-element.14) | copy-start | bytes 344068
